TPU v7x, 32 devices: a whole 2x2x4 slice. The times are simulated.
32 devices in a mesh: band: 4 (over y, x), chan: 8 (over z, core).
Axes of the slice: x: 2, y: 2, z: 4, core: 2. Of those that a mesh axis runs over, the one named last changes fastest.
Arguments:
- coeffs: bfloat16 [2, 8, 1024, 4096], P(None, None, 'chan', 'band'), may hold values from -1100 to 1100, as said below
Outputs:
- coherence: float32 [1024, 1024], P('chan', 'band')
Inputs may be any that keep to these rules, and one draw needn't show every extreme that they name: `coeffs`: finite real and imaginary parts.
All inputs are finite; a program needn't handle non-finite values.
Results may differ from a plain program's by a relative error of at most 0.0003.
Values may be sent and summed in bfloat16 or wider, within the bound.
A program may use at most 192 MiB of HBM per device.

v0:
```python
import functools

import jax
import jax.numpy as jnp
from jax import lax
from jax.experimental import pallas as pl
from jax.experimental.pallas import tpu as pltpu
from jax.sharding import PartitionSpec as P

W = 16

epsilon = 1e-06

MESH = pl.DeviceIdType.MESH


def partner(index, size, offset):
    other = index
    bit = 1
    while bit < size:
        if offset & bit:
            other = other + (1 - 2 * ((index // bit) % 2)) * bit
        bit *= 2
    return other


def kernel(x_ref, out_ref, buf, sel, xb, xq, inv_col, inv_row, own_sem, send_sem, recv_sem):
    n = lax.axis_size("chan")
    me = lax.axis_index("chan")
    parts, tapers, own, wide = buf.shape[1:]
    bands, full, depth = xb.shape
    lanes = bands * W
    half = depth // 2
    tile = min(256, full)

    def window(device):
        return pl.ds(pl.multiple_of(device * lanes // wide * wide, wide), wide)

    barrier = pltpu.get_barrier_semaphore()
    for offset in range(1, n):
        pl.semaphore_signal(
            barrier, inc=1, device_id={"chan": partner(me, n, offset)}, device_id_type=MESH
        )

    local = pltpu.make_async_copy(
        x_ref.at[:, :, :, window(me)], buf.at[me], own_sem
    )
    local.start()
    pl.semaphore_wait(barrier, n - 1)

    copies = {}
    for offset in reversed(range(1, n)):
        peer = partner(me, n, offset)
        copies[offset] = pltpu.make_async_remote_copy(
            src_ref=x_ref.at[:, :, :, window(peer)],
            dst_ref=buf.at[me],
            send_sem=send_sem.at[offset],
            recv_sem=recv_sem.at[offset],
            device_id={"chan": peer},
            device_id_type=MESH,
        )
        copies[offset].start()

    row = lax.broadcasted_iota(jnp.int32, (wide, bands * half), 0) - (me * lanes) % wide
    col = lax.broadcasted_iota(jnp.int32, (wide, bands * half), 1)
    band, within = col // half, col % half
    for k in range(tapers):
        hit = (row == band * W + within - k * W) & (within // W == k)
        sel[k * wide : (k + 1) * wide, :] = jnp.where(hit, 1.0, 0.0).astype(jnp.bfloat16)

    def relayout(src):
        rows = pl.ds(pl.multiple_of(src * own, own), own)
        re = jnp.concatenate([buf[src, 0, k] for k in range(tapers)], axis=1)
        im = jnp.concatenate([buf[src, 1, k] for k in range(tapers)], axis=1)
        lane = lax.broadcasted_iota(jnp.int32, (own, 128), 1)
        power = jnp.ones((own, 128), jnp.float32)
        for b in range(bands):
            chosen = sel[:, b * half : (b + 1) * half]
            re_b = jnp.dot(re, chosen, preferred_element_type=jnp.float32)
            im_b = jnp.dot(im, chosen, preferred_element_type=jnp.float32)
            total = jnp.sum(re_b * re_b + im_b * im_b, axis=1, keepdims=True) + epsilon
            power = jnp.where(lane == b, total, power)
            xb[b, rows, :half] = re_b.astype(jnp.bfloat16)
            xb[b, rows, half:] = im_b.astype(jnp.bfloat16)
            xq[b, rows, :half] = im_b.astype(jnp.bfloat16)
            xq[b, rows, half:] = (-re_b).astype(jnp.bfloat16)
        inv_col[rows, :] = 1.0 / power

    local.wait()
    relayout(me)
    for offset in range(1, n):
        copies[offset].wait_recv()
        relayout(partner(me, n, offset))

    count = full // tile
    for i in range(count):
        turned = inv_col[i * tile : (i + 1) * tile, :].T
        inv_row[:, i * tile : (i + 1) * tile] = turned[:bands, :]

    contract = (((1,), (1,)), ((), ()))
    for i in range(count):
        row0 = i * tile

        def column(j, carry):
            col0 = pl.multiple_of(j * tile, tile)
            acc = jnp.zeros((tile, tile), jnp.float32)
            for b in range(bands):
                right = xb[b, pl.ds(col0, tile), :]
                re = lax.dot_general(
                    xb[b, row0 : row0 + tile, :], right, contract, preferred_element_type=jnp.float32
                )
                im = lax.dot_general(
                    xq[b, row0 : row0 + tile, :], right, contract, preferred_element_type=jnp.float32
                )
                acc += ((re * re + im * im) * inv_col[row0 : row0 + tile, b : b + 1]) * inv_row[
                    b : b + 1, pl.ds(col0, tile)
                ]
            out_ref[row0 : row0 + tile, pl.ds(col0, tile)] = acc
            out_ref[pl.ds(col0, tile), row0 : row0 + tile] = acc.T
            return carry

        lax.fori_loop(i, count, column, 0)

    for offset in range(1, n):
        copies[offset].wait_send()


def body(coeffs):
    parts, tapers, own, bins = coeffs.shape
    n = lax.axis_size("chan")
    groups = lax.axis_size("band")
    full = own * n
    lanes = bins // n
    wide = max(lanes, 128)
    bands = lanes // W
    depth = parts * tapers * W
    scale = jnp.float32(W * tapers / (bins // W * groups))
    partial_sum = pl.pallas_call(
        kernel,
        out_shape=jax.ShapeDtypeStruct((full, full), jnp.float32),
        in_specs=[pl.BlockSpec(memory_space=pl.ANY)],
        out_specs=pl.BlockSpec(memory_space=pltpu.VMEM),
        scratch_shapes=[
            pltpu.VMEM((n, parts, tapers, own, wide), jnp.bfloat16),
            pltpu.VMEM((tapers * wide, bands * tapers * W), jnp.bfloat16),
            pltpu.VMEM((bands, full, depth), jnp.bfloat16),
            pltpu.VMEM((bands, full, depth), jnp.bfloat16),
            pltpu.VMEM((full, 128), jnp.float32),
            pltpu.VMEM((bands, full), jnp.float32),
            pltpu.SemaphoreType.DMA,
            pltpu.SemaphoreType.DMA((n,)),
            pltpu.SemaphoreType.DMA((n,)),
        ],
        compiler_params=pltpu.CompilerParams(
            collective_id=0, has_side_effects=True, vmem_limit_bytes=48 * 1024 * 1024
        ),
    )(coeffs)
    summed = lax.psum_scatter(partial_sum, "band", scatter_dimension=1, tiled=True)
    summed = lax.psum_scatter(summed, "chan", scatter_dimension=0, tiled=True)
    share = full // groups
    row_global = lax.broadcasted_iota(jnp.int32, (own, share), 0) + lax.axis_index("chan") * own
    col_global = lax.broadcasted_iota(jnp.int32, (own, share), 1) + lax.axis_index("band") * share
    return jnp.where(row_global == col_global, jnp.float32(0.0), summed) * scale


def solution(mesh):
    return jax.shard_map(
        body,
        mesh=mesh,
        in_specs=(P(None, None, "chan", "band"),),
        out_specs=P("chan", "band"),
        check_vma=False,
    )
```

profile of v0, /device:TPU:0, one launch (start us, length us, event | category | flops | bytes accessed | tf_op | source)
XLA Modules:
  0.0 215.7 jit_solution(13916168141612939069)
XLA Ops:
  6.5 0.0 reduce-scatter.3.cloned.1.call-start
  6.5 111.0 %shard_map.17 = f32[1024,1024]{1,0:T(8,128)S(1)} custom-call(bf16[2,8,128,1024]{3,2,1,0:T(8,128)(2,1)} %x_ref.1), custom_call_target="tpu_custom_call" | custom-call | tf_op jit(solution)/shard_map/pallas_call | solution.py:138
  117.5 0.0 copy-start
  117.5 1.9 copy-done
  119.5 0.0 reduce-scatter.3.cloned.1.call-update
  119.5 0.0 reduce-scatter.5.cloned.1.call-start
  119.5 52.8 %reduce-scatter.3.cloned.1.call-done = f32[1024,256]{1,0:T(8,128)} async-done(((f32[1024,1024]{1,0:T(8,128)}), f32[1024,256]{1,0:T(8,128)}) %reduce-scatter.3.cloned.1.call-update) | async-done | bytes 1048592 | tf_op jit(solution)/shard_map/reduce_scatter | solution.py:158
  172.3 0.0 reduce-scatter.5.cloned.1.call-update
  172.4 34.8 %reduce-scatter.5.cloned.1.call-done = f32[128,256]{1,0:T(8,128)} async-done(((f32[1024,256]{1,0:T(8,128)}), f32[128,256]{1,0:T(8,128)}) %reduce-scatter.5.cloned.1.call-update) | async-done | bytes 131088 | tf_op jit(solution)/shard_map/reduce_scatter | solution.py:159
  207.2 1.6 select_multiply_fusion
  (2 shorter events, 0.0 us)
Async XLA Ops:
  6.5 165.8 %reduce-scatter.3.cloned.1.call-start = ((), (), s32[]{:S(2)}) async-start(), calls=%async_computation.2 | async-start | bytes 5242880 | tf_op jit(solution)/shard_map/reduce_scatter | solution.py:158
  117.5 1.9 copy-start
  119.5 87.7 %reduce-scatter.5.cloned.1.call-start = ((), (), s32[]{:S(2)}) async-start(), calls=%async_computation.3 | async-start | bytes 1179648 | tf_op jit(solution)/shard_map/reduce_scatter | solution.py:159
Sparse Core Ops, SparseCore 0:
  119.6 52.6 reduce-scatter.2
  174.6 32.5 reduce-scatter.4
where the time goes:
time: 216 us
  Pallas kernels  111 us (51%)
  waiting for transfers between devices  87.6 us (41%)
  between operations  13.4 us (6%)
    pallas_call x1, Pallas kernels, body(): pl.pallas_call(kernel, out_shape=jax.ShapeDtypeStruct((full, full), jnp.f...  111 us
    reduce_scatter x1, waiting for transfers between devices, body(): lax.psum_scatter(partial_sum, 'band', scatter_dimension=1, tiled=True)  52.8 us
    reduce_scatter x1, waiting for transfers between devices, body(): summed = lax.psum_scatter(summed, 'chan', scatter_dimension=0, tiled=True)  34.8 us
  transfers between devices with their start and end apart: 2, of which 2 were waited for; matrix products, arithmetic and copies ran while one was open for 0% of the time, Pallas kernels for 0%

commit v1 on v0

v1 whole, which is shorter than its diff:
```python
import jax
import jax.numpy as jnp
from jax import lax
from jax.experimental import pallas as pl
from jax.experimental.pallas import tpu as pltpu
from jax.sharding import PartitionSpec as P

W = 16
LANE = 128

epsilon = 1e-06

MESH = pl.DeviceIdType.MESH


def quarter(side, z):
    seen = z + side * (3 - 2 * z)
    far = seen // 2
    return far * seen + (1 - far) * (1 - seen)


def group(side, q):
    far = q // 2
    seen = far * q + (1 - far) * (1 - q)
    return seen + side * (3 - 2 * seen)


def kernel(
    scale,
    x_ref,
    out_ref,
    buf,
    sel,
    xb,
    xq,
    inv_col,
    inv_row,
    part,
    land,
    zsend,
    zland,
    fin,
    fland,
    coef_send,
    coef_recv,
    part_send,
    part_recv,
    z_send,
    z_recv,
    fin_send,
    fin_recv,
):
    n = lax.axis_size("chan")
    groups = lax.axis_size("band")
    me = lax.axis_index("chan")
    column = lax.axis_index("band")
    strips, parts, tapers, strip, lanes = buf.shape
    bands, full, depth = xb.shape
    half = depth // 2
    m = n // 4
    own = full // n
    splits = strips // 4
    rows = own // splits
    quad = strips // 2
    shares = groups // 4
    members = groups * m
    per = LANE // W

    z = lax.div(me, m)
    lane = lax.rem(me, m)
    side = lax.div(z, 2)
    is_hub = (z == 1) | (z == 2)
    member = lane * groups + column

    barrier = pltpu.get_barrier_semaphore()
    for g in range(groups):
        for c in range(n):
            if g or c:
                pl.semaphore_signal(
                    barrier,
                    inc=1,
                    device_id={"band": lax.rem(column + g, groups), "chan": lax.rem(me + c, n)},
                    device_id_type=MESH,
                )
    pl.semaphore_wait(barrier, n * groups - 1)

    def coef_copy(far, s, t):
        to_side = side + far * (1 - 2 * side)
        hub = m + to_side * m + t
        w = quarter(to_side, z) * splits + s
        src = x_ref.at[
            :, :, pl.ds(s * rows, rows), pl.ds(pl.multiple_of((hub - m) * lanes, LANE), lanes)
        ]
        dst = buf.at[w, :, :, pl.ds(pl.multiple_of(lane * rows, rows), rows), :]
        recv = coef_recv.at[w, lane]

        def remote():
            return pltpu.make_async_remote_copy(
                src_ref=src,
                dst_ref=dst,
                send_sem=coef_send.at[far, s, t],
                recv_sem=recv,
                device_id={"chan": hub},
                device_id_type=MESH,
            )

        return hub, remote, lambda: pltpu.make_async_copy(src, dst, recv)

    for far in range(2):
        for s in range(splits):
            for t in range(m):
                hub, remote, local = coef_copy(far, s, t)
                if far:
                    remote().start()
                else:
                    pl.when(hub != me)(lambda: remote().start())
                    pl.when(hub == me)(lambda: local().start())

    def reducer(w, c):
        cross = lax.div(w, quad) * (1 - lax.div(c, quad))
        return lax.rem(lax.rem(w, quad) + lax.rem(c, quad), quad) + quad * cross

    def part_copy(w, c, to):
        rel = lax.rem(member - to + members, members)
        return pltpu.make_async_remote_copy(
            src_ref=part.at[w, c],
            dst_ref=land.at[w, rel],
            send_sem=part_send.at[w, c],
            recv_sem=part_recv.at[w, rel],
            device_id={
                "band": lax.rem(to, groups),
                "chan": m + side * m + lax.div(to, groups),
            },
            device_id_type=MESH,
        )

    def role(w):
        turn = lax.rem(member, quad)
        cross = lax.div(member, quad)
        upper = lax.div(w, quad)
        place = lax.rem(w, quad)
        q = lax.rem(turn - place + quad, quad)
        c = q + quad * upper * (1 - cross)
        valid = ((cross == 0) & (q <= place)) | ((cross == 1) & (upper == 1))
        other = jnp.where(cross == 1, q + quad, w + quad)
        crossing = cross == 1
        sends = valid & (
            (~crossing & (upper == 0))
            | (crossing & ((w < other) | ((w == other) & (side == 1))))
        )
        keeps = valid & (
            (~crossing & (upper == 1))
            | (crossing & ((w > other) | ((w == other) & (side == 0))))
        )
        return c, other, crossing, valid, sends, keeps

    def z_copy(w, other):
        return pltpu.make_async_remote_copy(
            src_ref=zsend.at[w],
            dst_ref=zland.at[other],
            send_sem=z_send.at[w],
            recv_sem=z_recv.at[other],
            device_id={"chan": m + (1 - side) * m + lane},
            device_id_type=MESH,
        )

    def final_copies(w, c):
        for turned in range(2):
            row, col = (c, w) if turned else (w, c)
            zr, zc = group(side, lax.div(row, splits)), group(side, lax.div(col, splits))
            sr, sc = lax.rem(row, splits), lax.rem(col, splits)
            for t in range(m):
                for j in range(shares):
                    chan, band = zr * m + t, zc * shares + j
                    src = fin.at[w, turned, pl.ds(t * rows, rows), :]
                    dst = fland.at[sr, sc]

                    def remote():
                        return pltpu.make_async_remote_copy(
                            src_ref=src,
                            dst_ref=dst,
                            send_sem=fin_send.at[w, turned, t, j],
                            recv_sem=fin_recv.at[sr, sc],
                            device_id={"band": band, "chan": chan},
                            device_id_type=MESH,
                        )

                    def local():
                        return pltpu.make_async_copy(src, dst, fin_recv.at[sr, sc])

                    mine = (chan == me) & (band == column)
                    wanted = (w != c) if turned else True
                    yield wanted, mine, remote, local

    def relayout(w):
        rows_w = pl.ds(pl.multiple_of(w * strip, strip), strip)
        at = lax.broadcasted_iota(jnp.int32, (strip, LANE), 1)
        power = jnp.ones((strip, LANE), jnp.float32)
        for v in range(lanes // LANE):
            window = slice(v * LANE, (v + 1) * LANE)
            both = jnp.concatenate(
                [
                    jnp.concatenate([buf[w, p, k, :, window] for k in range(tapers)], axis=1)
                    for p in range(parts)
                ],
                axis=0,
            )
            for d in range(per // 2):
                chosen = sel[:, 2 * d * half : 2 * (d + 1) * half]
                picked = jnp.dot(both, chosen, preferred_element_type=jnp.float32)
                for e in range(2):
                    b = v * per + 2 * d + e
                    re = picked[:strip, e * half : (e + 1) * half]
                    im = picked[strip:, e * half : (e + 1) * half]
                    total = jnp.sum(re * re + im * im, axis=1, keepdims=True) + epsilon
                    power = jnp.where(at == b, total, power)
                    xb[b, rows_w, :half] = re.astype(jnp.bfloat16)
                    xb[b, rows_w, half:] = im.astype(jnp.bfloat16)
                    xq[b, :, :half] = im.astype(jnp.bfloat16)
                    xq[b, :, half:] = (-re).astype(jnp.bfloat16)
        inverse = 1.0 / power
        inv_col[...] = inverse
        inv_row[:, pl.ds(pl.multiple_of(w * strip, strip), strip)] = inverse.T[:bands, :]

    contract = (((1,), (1,)), ((), ()))

    def gram(w):
        rows_w = pl.ds(pl.multiple_of(w * strip, strip), strip)

        def pair(v, carry):
            cols = pl.ds(pl.multiple_of(v * 2 * strip, 2 * strip), 2 * strip)
            acc = jnp.zeros((strip, 2 * strip), jnp.float32)
            for b in range(bands):
                left = jnp.concatenate([xb[b, rows_w, :], xq[b]], axis=0)
                both = lax.dot_general(
                    left, xb[b, cols, :], contract, preferred_element_type=jnp.float32
                )
                re, im = both[:strip], both[strip:]
                acc += ((re * re + im * im) * inv_col[:, b : b + 1]) * inv_row[b : b + 1, cols]
            for e in range(2):
                part[w, 2 * v + e] = acc[:, e * strip : (e + 1) * strip]
            for e in range(2):
                c = 2 * v + e
                to = reducer(w, c)

                @pl.when((c <= w) & (to != member))
                def _():
                    part_copy(w, c, to).start()

            return carry

        lax.fori_loop(0, lax.div(w, 2) + 1, pair, 0)

    def reduce(w):
        c, other, crossing, valid, sends, keeps = role(w)

        @pl.when(valid)
        def _():
            for rel in range(1, members):
                pltpu.make_async_copy(land.at[w, rel], land.at[w, rel], part_recv.at[w, rel]).wait()
            total = part[w, c]
            for rel in range(1, members):
                total += land[w, rel]

            @pl.when(sends & crossing)
            def _():
                zsend[w] = total.T

            @pl.when(sends & ~crossing)
            def _():
                zsend[w] = total

            @pl.when(sends)
            def _():
                z_copy(w, other).start()

            @pl.when(keeps)
            def _():
                pltpu.make_async_copy(zland.at[w], zland.at[w], z_recv.at[w]).wait()
                whole = total + zland[w]
                fin[w, 0] = whole
                fin[w, 1] = whole.T
                for wanted, mine, remote, local in final_copies(w, c):
                    pl.when(wanted & ~mine)(lambda: remote().start())
                    pl.when(wanted & mine)(lambda: local().start())

    @pl.when(is_hub)
    def _():
        row = lax.broadcasted_iota(jnp.int32, (LANE, per * half), 0)
        col = lax.broadcasted_iota(jnp.int32, (LANE, per * half), 1)
        band, within = col // half, col % half
        for k in range(tapers):
            hit = (row == band * W + within - k * W) & (within // W == k)
            sel[k * LANE : (k + 1) * LANE, :] = jnp.where(hit, 1.0, 0.0).astype(jnp.bfloat16)

        def step(w, carry):
            for t in range(m):
                dst = buf.at[w, :, :, pl.ds(t * rows, rows), :]
                pltpu.make_async_copy(dst, dst, coef_recv.at[w, t]).wait()
            relayout(w)
            gram(w)
            pl.when(w > 0)(lambda: reduce(w - 1))
            return carry

        lax.fori_loop(0, strips, step, 0)
        reduce(strips - 1)

        def drain(w, carry):
            def tile(c, carry):
                to = reducer(w, c)
                pl.when(to != member)(lambda: part_copy(w, c, to).wait_send())
                return carry

            lax.fori_loop(0, w + 1, tile, 0)
            c, other, crossing, valid, sends, keeps = role(w)
            pl.when(sends)(lambda: z_copy(w, other).wait_send())

            @pl.when(keeps)
            def _():
                for wanted, mine, remote, local in final_copies(w, c):
                    pl.when(wanted & ~mine)(lambda: remote().wait_send())

            return carry

        lax.fori_loop(0, strips, drain, 0)

    for far in range(2):
        for s in range(splits):
            for t in range(m):
                hub, remote, local = coef_copy(far, s, t)
                if far:
                    remote().wait_send()
                else:
                    pl.when(hub != me)(lambda: remote().wait_send())

    width = out_ref.shape[1]
    here = lax.rem(column, shares)
    per_share = m // shares
    for s in range(splits):
        for sc in range(splits):
            pltpu.make_async_copy(fland.at[s, sc], fland.at[s, sc], fin_recv.at[s, sc]).wait()
        choice = None
        for j in range(shares):
            pieces = [
                fland[s, sc, :, t * rows : (t + 1) * rows]
                for t in range(j * per_share, (j + 1) * per_share)
                for sc in range(splits)
            ]
            value = jnp.concatenate(pieces, axis=1)
            choice = value if choice is None else jnp.where(here == j, value, choice)
        row = lax.broadcasted_iota(jnp.int32, (rows, width), 0) + (me * own + s * rows)
        col = lax.broadcasted_iota(jnp.int32, (rows, width), 1) + column * width
        out_ref[s * rows : (s + 1) * rows, :] = jnp.where(row == col, 0.0, choice) * scale


def body(coeffs):
    parts, tapers, own, bins = coeffs.shape
    n = lax.axis_size("chan")
    groups = lax.axis_size("band")
    full = own * n
    m = n // 4
    hubs = 2 * m
    lanes = bins // hubs
    bands = lanes // W
    depth = parts * tapers * W
    strip = LANE
    strips = full // strip
    splits = strips // 4
    rows = own // splits
    members = groups * m
    shares = groups // 4
    scale = W * tapers / (bins // W * groups)
    dma = pltpu.SemaphoreType.DMA

    def run(*refs):
        kernel(scale, *refs)

    return pl.pallas_call(
        run,
        out_shape=jax.ShapeDtypeStruct((own, full // groups), jnp.float32),
        in_specs=[pl.BlockSpec(memory_space=pl.ANY)],
        out_specs=pl.BlockSpec(memory_space=pltpu.VMEM),
        scratch_shapes=[
            pltpu.VMEM((strips, parts, tapers, strip, lanes), jnp.bfloat16),
            pltpu.VMEM((tapers * LANE, LANE // W * depth // 2), jnp.bfloat16),
            pltpu.VMEM((bands, full, depth), jnp.bfloat16),
            pltpu.VMEM((bands, strip, depth), jnp.bfloat16),
            pltpu.VMEM((strip, LANE), jnp.float32),
            pltpu.VMEM((bands, full), jnp.float32),
            pltpu.VMEM((strips, strips, strip, strip), jnp.float32),
            pltpu.VMEM((strips, members, strip, strip), jnp.float32),
            pltpu.VMEM((strips, strip, strip), jnp.float32),
            pltpu.VMEM((strips, strip, strip), jnp.float32),
            pltpu.VMEM((strips, 2, strip, strip), jnp.float32),
            pltpu.VMEM((splits, splits, rows, strip), jnp.float32),
            dma((2, splits, m)),
            dma((strips, m)),
            dma((strips, strips)),
            dma((strips, members)),
            dma((strips,)),
            dma((strips,)),
            dma((strips, 2, m, shares)),
            dma((splits, splits)),
        ],
        compiler_params=pltpu.CompilerParams(
            collective_id=0, has_side_effects=True, vmem_limit_bytes=56 * 1024 * 1024
        ),
    )(coeffs)


def solution(mesh):
    return jax.shard_map(
        body,
        mesh=mesh,
        in_specs=(P(None, None, "chan", "band"),),
        out_specs=P("chan", "band"),
        check_vma=False,
    )
```

time: 216 us -> 120 us (0.56)
  the two profiles are of different devices: /device:TPU:0 before, /device:TPU:31 now
where the time goes in v1:
time: 120 us
  Pallas kernels  118 us (98%)
  local copies, waits for them, and re-layouts  1.57 us (1%)
    pallas_call x1, Pallas kernels, body(): pl.pallas_call(run, out_shape=jax.ShapeDtypeStruct((own, full // groups),...  118 us

profile of v1, /device:TPU:31, one launch (start us, length us, event | category | flops | bytes accessed | tf_op | source)
XLA Modules:
  0.0 119.8 jit_solution(11499518631390577724)
XLA Ops:
  0.0 118.2 %shard_map.17 = f32[128,256]{1,0:T(8,128)} custom-call(bf16[2,8,128,1024]{3,2,1,0:T(8,128)(2,1)} %refs_0_.1), custom_call_target="tpu_custom_call" | custom-call | tf_op jit(solution)/shard_map/pallas_call | solution.py:378
  118.2 1.6 %copy.3 = f32[128,256]{1,0:T(8,128)} copy(f32[128,256]{1,0:T(8,128)} %shard_map.17) | data formatting | bytes 262144

commit v2 on v1

v2 whole, which is shorter than its diff:
```python
import jax
import jax.numpy as jnp
from jax import lax
from jax.experimental import pallas as pl
from jax.experimental.pallas import tpu as pltpu
from jax.sharding import PartitionSpec as P

W = 16
LANE = 128
SUBS = 2

epsilon = 1e-06

MESH = pl.DeviceIdType.MESH


def quarter(side, z):
    seen = z + side * (3 - 2 * z)
    far = seen // 2
    return far * seen + (1 - far) * (1 - seen)


def group(side, q):
    far = q // 2
    seen = far * q + (1 - far) * (1 - q)
    return seen + side * (3 - 2 * seen)


def kernel(
    scale,
    x_ref,
    out_ref,
    buf,
    sel,
    xb,
    xq,
    inv_col,
    inv_row,
    part,
    land,
    total,
    zsend,
    zland,
    fin,
    fland,
    coef_send,
    coef_recv,
    part_send,
    part_recv,
    z_send,
    z_recv,
    fin_send,
    fin_recv,
    ready,
    met,
    go,
):
    n = lax.axis_size("chan")
    groups = lax.axis_size("band")
    me = lax.axis_index("chan")
    column = lax.axis_index("band")
    strips, parts, tapers, strip, lanes = buf.shape
    splits, subs, rows = fland.shape[1:4]
    bands, full, depth = xb.shape
    half = depth // 2
    m = n // 4
    own = full // n
    quad = strips // 2
    shares = groups // 4
    members = groups * m
    per = LANE // W
    slab = strip // subs

    z = lax.div(me, m)
    lane = lax.rem(me, m)
    side = lax.div(z, 2)
    is_hub = (z == 1) | (z == 2)
    member = lane * groups + column
    mine = quarter(side, lax.div(column, shares)) * splits + lane
    reduces = (lane < splits) & (lax.rem(column, shares) == 0)

    barrier = pltpu.get_barrier_semaphore()
    envoy = m + 1
    is_envoy = me == envoy

    @pl.when(is_hub)
    def _():
        for c in range(1, n):
            pl.semaphore_signal(
                barrier, inc=1, device_id={"chan": lax.rem(me + c, n)}, device_id_type=MESH
            )

    @pl.when(is_envoy)
    def _():
        for g in range(1, groups):
            pl.semaphore_signal(
                barrier,
                inc=1,
                device_id={"band": lax.rem(column + g, groups)},
                device_id_type=MESH,
            )

    pl.semaphore_wait(
        barrier, 2 * m - is_hub.astype(jnp.int32) + is_envoy.astype(jnp.int32) * (groups - 1)
    )

    def coef_copy(far, s, i, t):
        to_side = side + far * (1 - 2 * side)
        hub = m + to_side * m + t
        w = quarter(to_side, z) * splits + s
        src = x_ref.at[
            :,
            :,
            pl.ds((s * subs + i) * rows, rows),
            pl.ds(pl.multiple_of((hub - m) * lanes, LANE), lanes),
        ]
        dst = buf.at[w, :, :, pl.ds(pl.multiple_of(i * slab + lane * rows, rows), rows), :]
        recv = coef_recv.at[w, i, lane]

        def remote():
            return pltpu.make_async_remote_copy(
                src_ref=src,
                dst_ref=dst,
                send_sem=coef_send.at[far, s, i, t],
                recv_sem=recv,
                device_id={"chan": hub},
                device_id_type=MESH,
            )

        return hub, remote, lambda: pltpu.make_async_copy(src, dst, recv)

    order = [
        (far, s, i, t) for far in range(2) for s in range(splits) for i in range(subs) for t in range(m)
    ]
    for far, s, i, t in order:
        hub, remote, local = coef_copy(far, s, i, t)
        if far:
            remote().start()
        else:
            pl.when(hub != me)(lambda: remote().start())
            pl.when(hub == me)(lambda: local().start())

    @pl.when(~is_hub)
    def _():
        pl.semaphore_signal(ready, inc=1, device_id={"chan": envoy}, device_id_type=MESH)

    def meet():
        @pl.when(is_envoy)
        def _():
            pl.semaphore_wait(ready, n - 2 * m)
            for g in range(1, groups):
                pl.semaphore_signal(
                    met,
                    inc=1,
                    device_id={"band": lax.rem(column + g, groups)},
                    device_id_type=MESH,
                )
            pl.semaphore_wait(met, groups - 1)
            for h in range(2 * m):
                if m + h != envoy:
                    pl.semaphore_signal(go, inc=1, device_id={"chan": m + h}, device_id_type=MESH)

        @pl.when(~is_envoy)
        def _():
            pl.semaphore_wait(go, 1)

    def place(to_side, c):
        band = group(to_side, lax.div(c, splits)) * shares
        at = lax.rem(c, splits)
        return band, m + to_side * m + at, at * groups + band

    def part_copy(w, c):
        band, chan, to = place(side, c)
        return pltpu.make_async_remote_copy(
            src_ref=part.at[w, c],
            dst_ref=land.at[w, lax.rem(member - to + members, members)],
            send_sem=part_send.at[w, c],
            recv_sem=part_recv.at[w],
            device_id={"band": band, "chan": chan},
            device_id_type=MESH,
        )

    def role(w):
        c = mine
        valid = reduces & (c <= w)
        upper = w >= quad
        crossing = upper & (c < quad)
        even = w == c + quad
        sends = valid & (
            (w < quad) | (crossing & ((w < c + quad) | (even & (side == 1))))
        )
        keeps = valid & (
            (c >= quad) | (crossing & ((w > c + quad) | (even & (side == 0))))
        )
        return crossing, valid, sends, keeps

    def z_copy(w):
        crossed = lax.div(w, quad)
        to = crossed * (w - quad) + (1 - crossed) * (mine + quad)
        slot = crossed * (mine + quad) + (1 - crossed) * (w + quad)
        band, chan, unused = place(1 - side, to)
        return pltpu.make_async_remote_copy(
            src_ref=zsend.at[w],
            dst_ref=zland.at[slot],
            send_sem=z_send.at[w],
            recv_sem=z_recv.at[slot],
            device_id={"band": band, "chan": chan},
            device_id_type=MESH,
        )

    def final_copies(w):
        for turned in range(2):
            row, col = (mine, w) if turned else (w, mine)
            zr, zc = group(side, lax.div(row, splits)), group(side, lax.div(col, splits))
            sr, sc = lax.rem(row, splits), lax.rem(col, splits)
            for t in range(m):
                for j in range(shares):
                    chan, band = zr * m + t, zc * shares + j
                    src = fin.at[w, turned, :, t]
                    dst = fland.at[sr, sc]

                    def remote():
                        return pltpu.make_async_remote_copy(
                            src_ref=src,
                            dst_ref=dst,
                            send_sem=fin_send.at[w, turned, t, j],
                            recv_sem=fin_recv.at[sr, sc],
                            device_id={"band": band, "chan": chan},
                            device_id_type=MESH,
                        )

                    def local():
                        return pltpu.make_async_copy(src, dst, fin_recv.at[sr, sc])

                    here = (chan == me) & (band == column)
                    wanted = (w != mine) if turned else True
                    yield wanted, here, remote, local

    def relayout(w, i):
        rows_w = pl.ds(pl.multiple_of(w * strip + i * slab, slab), slab)
        at = lax.broadcasted_iota(jnp.int32, (slab, LANE), 1)
        power = jnp.ones((slab, LANE), jnp.float32)
        inside = pl.ds(pl.multiple_of(i * slab, slab), slab)
        for v in range(lanes // LANE):
            window = slice(v * LANE, (v + 1) * LANE)
            both = jnp.concatenate(
                [
                    jnp.concatenate([buf[w, p, k, inside, window] for k in range(tapers)], axis=1)
                    for p in range(parts)
                ],
                axis=0,
            )
            for d in range(per // 2):
                chosen = sel[:, 2 * d * half : 2 * (d + 1) * half]
                picked = jnp.dot(both, chosen, preferred_element_type=jnp.float32)
                for e in range(2):
                    b = v * per + 2 * d + e
                    re = picked[:slab, e * half : (e + 1) * half]
                    im = picked[slab:, e * half : (e + 1) * half]
                    sums = jnp.sum(re * re + im * im, axis=1, keepdims=True) + epsilon
                    power = jnp.where(at == b, sums, power)
                    xb[b, rows_w, :half] = re.astype(jnp.bfloat16)
                    xb[b, rows_w, half:] = im.astype(jnp.bfloat16)
                    xq[b, inside, :half] = im.astype(jnp.bfloat16)
                    xq[b, inside, half:] = (-re).astype(jnp.bfloat16)
        inv_col[inside, :] = 1.0 / power
        inv_row[:, pl.ds(pl.multiple_of(w * strip, strip), strip)] = inv_col[...].T[:bands, :]

    contract = (((1,), (1,)), ((), ()))

    def gram(w):
        rows_w = pl.ds(pl.multiple_of(w * strip, strip), strip)
        at = lax.div(column, shares)

        def pair(k, carry):
            pl.when((w == strips - 1) & (k == 3))(finish_early)
            seat = jnp.where(
                k == 0,
                3 - at,
                jnp.where(k == 1, lax.rem(at + 2, 4), jnp.where(k == 2, at + 1 - 2 * lax.rem(at, 2), at)),
            )
            v = quarter(side, seat)

            @pl.when(2 * v <= w)
            def _():
                cols = pl.ds(pl.multiple_of(v * 2 * strip, 2 * strip), 2 * strip)
                acc = jnp.zeros((strip, 2 * strip), jnp.float32)
                for b in range(bands):
                    left = jnp.concatenate([xb[b, rows_w, :], xq[b]], axis=0)
                    both = lax.dot_general(
                        left, xb[b, cols, :], contract, preferred_element_type=jnp.float32
                    )
                    re, im = both[:strip], both[strip:]
                    acc += ((re * re + im * im) * inv_col[:, b : b + 1]) * inv_row[b : b + 1, cols]
                for e in range(2):
                    part[w, 2 * v + e] = acc[:, e * strip : (e + 1) * strip]
                for e in range(2):
                    c = 2 * v + e
                    to = place(side, c)[2]
                    pl.when((c <= w) & (to != member))(lambda: part_copy(w, c).start())

            return carry

        lax.fori_loop(0, 4, pair, 0)

    def reduce(w):
        crossing, valid, sends, keeps = role(w)

        @pl.when(valid)
        def _():
            every = land.at[w, pl.ds(1, members - 1)]
            pltpu.make_async_copy(every, every, part_recv.at[w]).wait()
            summed = part[w, mine]
            for rel in range(1, members):
                summed += land[w, rel]

            @pl.when(sends & crossing)
            def _():
                zsend[w] = summed.T

            @pl.when(sends & ~crossing)
            def _():
                zsend[w] = summed

            @pl.when(sends)
            def _():
                z_copy(w).start()

            @pl.when(keeps)
            def _():
                total[w] = summed

    def finish(w):
        crossing, valid, sends, keeps = role(w)

        @pl.when(keeps)
        def _():
            pltpu.make_async_copy(zland.at[w], zland.at[w], z_recv.at[w]).wait()
            whole = total[w] + zland[w]
            turned = whole.T
            fin[w, 0] = whole.reshape(subs, m, rows, strip)
            fin[w, 1] = turned.reshape(subs, m, rows, strip)
            for wanted, here, remote, local in final_copies(w):
                pl.when(wanted & ~here)(lambda: remote().start())
                pl.when(wanted & here)(lambda: local().start())

    def finish_early():
        lax.fori_loop(quad, strips - 1, lambda w, carry: (finish(w), carry)[1], 0)

    def drain_parts(w, carry):
        def tile(c, carry):
            @pl.when(place(side, c)[2] != member)
            def _():
                part_copy(w, c).wait_send()

            return carry

        lax.fori_loop(0, w + 1, tile, 0)
        return carry

    def drain_tiles(w, carry):
        crossing, valid, sends, keeps = role(w)
        pl.when(sends)(lambda: z_copy(w).wait_send())

        @pl.when(keeps)
        def _():
            for wanted, here, remote, local in final_copies(w):
                pl.when(wanted & ~here)(lambda: remote().wait_send())

        return carry

    @pl.when(is_hub)
    def _():
        row = lax.broadcasted_iota(jnp.int32, (LANE, per * half), 0)
        col = lax.broadcasted_iota(jnp.int32, (LANE, per * half), 1)
        band, within = col // half, col % half
        for k in range(tapers):
            hit = (row == band * W + within - k * W) & (within // W == k)
            sel[k * LANE : (k + 1) * LANE, :] = jnp.where(hit, 1.0, 0.0).astype(jnp.bfloat16)

        def step(h, carry):
            w, i = lax.div(h, subs), lax.rem(h, subs)
            for t in range(m):
                dst = buf.at[w, :, :, pl.ds(pl.multiple_of(i * slab + t * rows, rows), rows), :]
                pltpu.make_async_copy(dst, dst, coef_recv.at[w, i, t]).wait()
            relayout(w, i)

            @pl.when(i == subs - 1)
            def _():
                pl.when(w > 0)(lambda: reduce(w - 1))
                gram(w)

            return carry

        meet()
        lax.fori_loop(0, strips * subs, step, 0)
        lax.fori_loop(0, strips - 1, drain_parts, 0)
        reduce(strips - 1)
        finish(strips - 1)
        drain_parts(strips - 1, 0)
        lax.fori_loop(0, strips, drain_tiles, 0)

    for far, s, i, t in order:
        hub, remote, local = coef_copy(far, s, i, t)
        if far:
            remote().wait_send()
        else:
            pl.when(hub != me)(lambda: remote().wait_send())

    width = out_ref.shape[1]
    here = lax.rem(column, shares)
    per_share = m // shares
    deep = subs * rows
    for s in range(splits):
        for sc in range(splits):
            pltpu.make_async_copy(fland.at[s, sc], fland.at[s, sc], fin_recv.at[s, sc]).wait()
        choice = None
        for j in range(shares):
            pieces = [
                fland[s, sc, :, :, i * slab + t * rows : i * slab + (t + 1) * rows].reshape(deep, rows)
                for t in range(j * per_share, (j + 1) * per_share)
                for sc in range(splits)
                for i in range(subs)
            ]
            value = jnp.concatenate(pieces, axis=1)
            choice = value if choice is None else jnp.where(here == j, value, choice)
        row = lax.broadcasted_iota(jnp.int32, (deep, width), 0) + (me * own + s * deep)
        col = lax.broadcasted_iota(jnp.int32, (deep, width), 1) + column * width
        out_ref[s * deep : (s + 1) * deep, :] = jnp.where(row == col, 0.0, choice) * scale


def body(coeffs):
    parts, tapers, own, bins = coeffs.shape
    n = lax.axis_size("chan")
    groups = lax.axis_size("band")
    full = own * n
    m = n // 4
    hubs = 2 * m
    lanes = bins // hubs
    bands = lanes // W
    depth = parts * tapers * W
    strip = LANE
    strips = full // strip
    splits = strips // 4
    subs = min(SUBS, own // splits // 16)
    rows = own // splits // subs
    slab = strip // subs
    members = groups * m
    shares = groups // 4
    scale = W * tapers / (bins // W * groups)
    dma = pltpu.SemaphoreType.DMA

    def run(*refs):
        kernel(scale, *refs)

    return pl.pallas_call(
        run,
        out_shape=pltpu.VMEM((own, full // groups), jnp.float32),
        in_specs=[pl.BlockSpec(memory_space=pl.ANY)],
        out_specs=pl.BlockSpec(memory_space=pltpu.VMEM),
        scratch_shapes=[
            pltpu.VMEM((strips, parts, tapers, strip, lanes), jnp.bfloat16),
            pltpu.VMEM((tapers * LANE, LANE // W * depth // 2), jnp.bfloat16),
            pltpu.VMEM((bands, full, depth), jnp.bfloat16),
            pltpu.VMEM((bands, strip, depth), jnp.bfloat16),
            pltpu.VMEM((strip, LANE), jnp.float32),
            pltpu.VMEM((bands, full), jnp.float32),
            pltpu.VMEM((strips, strips, strip, strip), jnp.float32),
            pltpu.VMEM((strips, members, strip, strip), jnp.float32),
            pltpu.VMEM((strips, strip, strip), jnp.float32),
            pltpu.VMEM((strips, strip, strip), jnp.float32),
            pltpu.VMEM((strips, strip, strip), jnp.float32),
            pltpu.VMEM((strips, 2, subs, m, rows, strip), jnp.float32),
            pltpu.VMEM((splits, splits, subs, rows, strip), jnp.float32),
            dma((2, splits, subs, m)),
            dma((strips, subs, m)),
            dma((strips, strips)),
            dma((strips,)),
            dma((strips,)),
            dma((strips,)),
            dma((strips, 2, m, shares)),
            dma((splits, splits)),
            pltpu.SemaphoreType.REGULAR,
            pltpu.SemaphoreType.REGULAR,
            pltpu.SemaphoreType.REGULAR,
        ],
        compiler_params=pltpu.CompilerParams(
            collective_id=0, has_side_effects=True, vmem_limit_bytes=56 * 1024 * 1024
        ),
    )(coeffs)


def solution(mesh):
    return jax.shard_map(
        body,
        mesh=mesh,
        in_specs=(P(None, None, "chan", "band"),),
        out_specs=P("chan", "band"),
        check_vma=False,
    )
```

time: 120 us -> 112 us (0.933)
  the two profiles are of different devices: /device:TPU:31 before, /device:TPU:0 now
where the time goes in v2:
time: 112 us; the launch traced here: 111 us
  Pallas kernels  110 us (98%)
    pallas_call x1, Pallas kernels, body(): pl.pallas_call(run, out_shape=pltpu.VMEM((own, full // groups), jnp.float...  110 us

profile of v2, /device:TPU:0, one launch (start us, length us, event | category | flops | bytes accessed | tf_op | source)
XLA Modules:
  0.0 111.0 jit_solution(7989024103160891299)
XLA Ops:
  0.0 110.3 %shard_map.17 = f32[128,256]{1,0:T(8,128)S(1)} custom-call(bf16[2,8,128,1024]{3,2,1,0:T(8,128)(2,1)} %refs_0_.1), custom_call_target="tpu_custom_call" | custom-call | tf_op jit(solution)/shard_map/pallas_call | solution.py:456
  110.3 0.7 copy.3

commit v3 on v2

v3 whole, which is shorter than its diff:
```python
import jax
import jax.numpy as jnp
from jax import lax
from jax.experimental import pallas as pl
from jax.experimental.pallas import tpu as pltpu
from jax.sharding import PartitionSpec as P

W = 16
LANE = 128
SUBS = 2

epsilon = 1e-06

MESH = pl.DeviceIdType.MESH


def quarter(side, z):
    seen = z + side * (3 - 2 * z)
    far = seen // 2
    return far * seen + (1 - far) * (1 - seen)


def group(side, q):
    far = q // 2
    seen = far * q + (1 - far) * (1 - q)
    return seen + side * (3 - 2 * seen)


def kernel(
    scale,
    x_ref,
    out_ref,
    buf,
    sel,
    xb,
    left,
    inv_own,
    inv_col,
    inv_row,
    part,
    land,
    fin,
    fland,
    coef_send,
    coef_recv,
    part_send,
    part_recv,
    fin_send,
    fin_recv,
    ready,
    met,
    go,
):
    n = lax.axis_size("chan")
    groups = lax.axis_size("band")
    me = lax.axis_index("chan")
    column = lax.axis_index("band")
    strips, windows, parts, tapers, strip, unused = buf.shape
    lanes = windows * LANE
    splits = fland.shape[1]
    bands, full, depth = xb.shape
    half = depth // 2
    m = n // 4
    own = full // n
    quad = strips // 2
    shares = groups // 4
    members = groups * m
    per = LANE // W
    deep = strip // m
    subs = part.shape[2]
    slab = strip // subs
    rows = deep // subs

    z = lax.div(me, m)
    lane = lax.rem(me, m)
    side = lax.div(z, 2)
    is_hub = (z == 1) | (z == 2)
    member = lane * groups + column
    mine = quarter(side, lax.div(column, shares)) * splits + lane
    reduces = (lane < splits) & (lax.rem(column, shares) == 0)

    barrier = pltpu.get_barrier_semaphore()
    envoy = m + 1
    is_envoy = me == envoy

    @pl.when(is_hub)
    def _():
        for c in range(1, n):
            pl.semaphore_signal(
                barrier, inc=1, device_id={"chan": lax.rem(me + c, n)}, device_id_type=MESH
            )

    @pl.when(is_envoy)
    def _():
        for g in range(1, groups):
            pl.semaphore_signal(
                barrier,
                inc=1,
                device_id={"band": lax.rem(column + g, groups)},
                device_id_type=MESH,
            )

    pl.semaphore_wait(
        barrier, 2 * m - is_hub.astype(jnp.int32) + is_envoy.astype(jnp.int32) * (groups - 1)
    )

    def coef_copy(far, s, v, i, t):
        to_side = side + far * (1 - 2 * side)
        hub = m + to_side * m + t
        w = quarter(to_side, z) * splits + s
        first = (hub - m) * lanes + v * LANE
        src = x_ref.at[
            :, :, pl.ds(s * deep + i * rows, rows), pl.ds(pl.multiple_of(first, LANE), LANE)
        ]
        dst = buf.at[w, v, :, :, pl.ds(pl.multiple_of(i * slab + lane * rows, rows), rows), :]
        recv = coef_recv.at[w, v, i]

        def remote():
            return pltpu.make_async_remote_copy(
                src_ref=src,
                dst_ref=dst,
                send_sem=coef_send.at[far, t],
                recv_sem=recv,
                device_id={"chan": hub},
                device_id_type=MESH,
            )

        return hub, remote, lambda: pltpu.make_async_copy(src, dst, recv)

    order = [
        (far, s, v, i, t)
        for far in range(2)
        for s in range(splits)
        for v in range(windows)
        for i in range(subs)
        for t in range(m)
    ]
    for far, *chunk in order:
        hub, remote, local = coef_copy(far, *chunk)
        if far:
            remote().start()
        else:
            pl.when(hub != me)(lambda: remote().start())
            pl.when(hub == me)(lambda: local().start())

    @pl.when(~is_hub)
    def _():
        pl.semaphore_signal(ready, inc=1, device_id={"chan": envoy}, device_id_type=MESH)

    def meet():
        @pl.when(is_envoy)
        def _():
            pl.semaphore_wait(ready, n - 2 * m)
            for g in range(1, groups):
                pl.semaphore_signal(
                    met,
                    inc=1,
                    device_id={"band": lax.rem(column + g, groups)},
                    device_id_type=MESH,
                )
            pl.semaphore_wait(met, groups - 1)
            for h in range(2 * m):
                if m + h != envoy:
                    pl.semaphore_signal(go, inc=1, device_id={"chan": m + h}, device_id_type=MESH)

        @pl.when(~is_envoy)
        def _():
            pl.semaphore_wait(go, 1)

    last = strips - 1

    def place(c):
        band = group(side, lax.div(c, splits)) * shares
        at = lax.rem(c, splits)
        return band, m + side * m + at, at * groups + band

    def part_copy(w, c, i):
        band, chan, to = place(c)
        return pltpu.make_async_remote_copy(
            src_ref=part.at[w, c, i],
            dst_ref=land.at[w, lax.rem(member - to + members, members), i],
            send_sem=part_send.at[c],
            recv_sem=part_recv.at[w],
            device_id={"band": band, "chan": chan},
            device_id_type=MESH,
        )

    def final_copies(w):
        for turned in range(2):
            row, col = (mine, w) if turned else (w, mine)
            zr, zc = group(side, lax.div(row, splits)), group(side, lax.div(col, splits))
            sr, sc = lax.rem(row, splits), lax.rem(col, splits)
            for t in range(m):
                for j in range(shares):
                    chan, band = zr * m + t, zc * shares + j
                    src = fin.at[w, turned, pl.ds(t * deep, deep), :]
                    dst = fland.at[side, sr, sc]

                    def remote():
                        return pltpu.make_async_remote_copy(
                            src_ref=src,
                            dst_ref=dst,
                            send_sem=fin_send.at[w, turned, j],
                            recv_sem=fin_recv,
                            device_id={"band": band, "chan": chan},
                            device_id_type=MESH,
                        )

                    def local():
                        return pltpu.make_async_copy(src, dst, fin_recv)

                    here = (chan == me) & (band == column)
                    wanted = (w != mine) if turned else True
                    yield row >= quad, wanted, here, remote, local

    def relayout(w, v, i):
        at = lax.broadcasted_iota(jnp.int32, (slab, LANE), 1)
        power = jnp.ones((slab, LANE), jnp.float32)
        spans = [pl.ds(pl.multiple_of(t * deep + i * rows, rows), rows) for t in range(m)]
        homes = [pl.ds(pl.multiple_of(w * strip + t * deep + i * rows, rows), rows) for t in range(m)]
        chunk = pl.ds(pl.multiple_of(i * slab, slab), slab)
        both = jnp.concatenate(
            [
                jnp.concatenate([buf[w, v, p, k, chunk] for k in range(tapers)], axis=1)
                for p in range(parts)
            ],
            axis=0,
        )
        for d in range(per // 2):
            chosen = sel[:, 2 * d * half : 2 * (d + 1) * half]
            picked = jnp.dot(both, chosen, preferred_element_type=jnp.float32)
            for e in range(2):
                near = 2 * d + e
                b = v * per + near
                re = picked[:slab, e * half : (e + 1) * half]
                im = picked[slab:, e * half : (e + 1) * half]
                sums = jnp.sum(re * re + im * im, axis=1, keepdims=True) + epsilon
                power = jnp.where(at == near, sums, power)
                left[near, :slab, :half] = re.astype(jnp.bfloat16)
                left[near, :slab, half:] = im.astype(jnp.bfloat16)
                left[near, slab:, :half] = im.astype(jnp.bfloat16)
                left[near, slab:, half:] = (-re).astype(jnp.bfloat16)
                for t in range(m):
                    segment = slice(t * rows, (t + 1) * rows)
                    xb[b, homes[t], :half] = re[segment].astype(jnp.bfloat16)
                    xb[b, homes[t], half:] = im[segment].astype(jnp.bfloat16)
        inverse = 1.0 / power
        inv_own[...] = inverse
        for t in range(m):
            inv_col[spans[t], :] = inverse[t * rows : (t + 1) * rows]
        inv_row[
            pl.ds(pl.multiple_of(v * per, per), per), pl.ds(pl.multiple_of(w * strip, strip), strip)
        ] = inv_col[...].T[:per, :]

    contract = (((1,), (1,)), ((), ()))

    def gram(w, v, i):
        at = lax.div(column, shares)

        def pair(k, carry):
            seat = jnp.where(
                k == 0,
                3 - at,
                jnp.where(k == 1, lax.rem(at + 2, 4), jnp.where(k == 2, at + 1 - 2 * lax.rem(at, 2), at)),
            )
            u = quarter(side, seat)

            @pl.when(2 * u <= w)
            def _():
                cols = pl.ds(pl.multiple_of(u * 2 * strip, 2 * strip), 2 * strip)
                scales = inv_row[pl.ds(pl.multiple_of(v * per, per), per), cols]
                acc = jnp.zeros((slab, 2 * strip), jnp.float32)
                for d in range(per):
                    b = v * per + d
                    both = lax.dot_general(
                        left[d], xb[b, cols, :], contract, preferred_element_type=jnp.float32
                    )
                    re, im = both[:slab], both[slab:]
                    acc += ((re * re + im * im) * inv_own[:, d : d + 1]) * scales[d : d + 1, :]

                for e in range(2):
                    c = 2 * u + e
                    here = acc[:, e * strip : (e + 1) * strip]
                    if windows == 1:
                        part[w, c, i] = here
                    else:

                        @pl.when(v == 0)
                        def _():
                            part[w, c, i] = here

                        @pl.when(v > 0)
                        def _():
                            part[w, c, i] += here

                for e in range(2):
                    c = 2 * u + e
                    to = place(c)[2]
                    pl.when((v == windows - 1) & (c <= w) & (to != member))(
                        lambda: part_copy(w, c, i).start()
                    )

            return carry

        lax.fori_loop(0, 4, pair, 0)

    def reduce(w):
        @pl.when(reduces & (mine <= w))
        def _():
            every = land.at[w, pl.ds(1, members - 1)]
            pltpu.make_async_copy(every, every, part_recv.at[w]).wait()
            for i in range(subs):
                summed = part[w, mine, i]
                for rel in range(1, members):
                    summed += land[w, rel, i]
                for t in range(m):
                    home = slice(t * deep + i * rows, t * deep + (i + 1) * rows)
                    fin[w, 0, home, :] = summed[t * rows : (t + 1) * rows]
            whole = fin[w, 0]
            turned = whole.T
            fin[w, 1] = turned

            @pl.when(w == mine)
            def _():
                row = lax.broadcasted_iota(jnp.int32, (strip, strip), 0) % deep // rows
                col = lax.broadcasted_iota(jnp.int32, (strip, strip), 1) % deep // rows
                fin[w, 0] = jnp.where(row < col, turned, whole)

            for crossing, wanted, here, remote, local in final_copies(w):
                now = wanted & (~crossing | (w == last))
                pl.when(now & ~here)(lambda: remote().start())
                pl.when(now & here)(lambda: local().start())

    def send_held(w, carry):
        @pl.when(reduces & (mine <= w))
        def _():
            for crossing, wanted, here, remote, local in final_copies(w):
                pl.when(wanted & crossing)(lambda: remote().start())

        return carry

    def drain_parts():
        for c in range(strips):

            @pl.when(place(c)[2] != member)
            def _():
                sent = part.at[pl.ds(c, strips - c), c]
                pltpu.make_async_copy(sent, sent, part_send.at[c]).wait()

    def drain_tiles(w, carry):
        @pl.when(reduces & (mine <= w))
        def _():
            for turned in range(2):
                row, col = (mine, w) if turned else (w, mine)
                ours = group(side, lax.div(row, splits)) == z
                for j in range(shares):
                    band = group(side, lax.div(col, splits)) * shares + j
                    here = ours & (band == column)
                    wanted = (w != mine) if turned else True
                    every = fin.at[w, turned]
                    others = fin.at[w, turned, pl.ds(0, strip - deep), :]
                    sem = fin_send.at[w, turned, j]
                    pl.when(wanted & ~here)(lambda: pltpu.make_async_copy(every, every, sem).wait())
                    pl.when(wanted & here)(lambda: pltpu.make_async_copy(others, others, sem).wait())

        return carry

    @pl.when(is_hub)
    def _():
        row = lax.broadcasted_iota(jnp.int32, (LANE, per * half), 0)
        col = lax.broadcasted_iota(jnp.int32, (LANE, per * half), 1)
        band, within = col // half, col % half
        for k in range(tapers):
            hit = (row == band * W + within - k * W) & (within // W == k)
            sel[k * LANE : (k + 1) * LANE, :] = jnp.where(hit, 1.0, 0.0).astype(jnp.bfloat16)

        def step(h, carry):
            w = lax.div(h, windows * subs)
            v = lax.rem(lax.div(h, subs), windows)
            i = lax.rem(h, subs)
            pl.when((w > 0) & (v == windows - 1) & (i == 0))(lambda: reduce(w - 1))
            dst = buf.at[w, v, :, :, pl.ds(pl.multiple_of(i * slab, slab), slab), :]
            pltpu.make_async_copy(dst, dst, coef_recv.at[w, v, i]).wait()
            relayout(w, v, i)
            gram(w, v, i)
            return carry

        meet()
        lax.fori_loop(0, strips * windows * subs, step, 0)
        lax.fori_loop(quad, last, send_held, 0)
        reduce(last)
        drain_parts()
        lax.fori_loop(0, strips, drain_tiles, 0)

    for far in range(2):
        for t in range(m):
            hub = m + (side + far * (1 - 2 * side)) * m + t
            sent = x_ref.at[:, :, :, pl.ds(pl.multiple_of((hub - m) * lanes, LANE), lanes)]

            @pl.when(hub != me)
            def _():
                pltpu.make_async_copy(sent, sent, coef_send.at[far, t]).wait()

    width = out_ref.shape[1]
    here = lax.rem(column, shares)
    per_share = m // shares
    pltpu.make_async_copy(fland, fland, fin_recv).wait()
    for s in range(splits):
        choice = None
        for j in range(shares):
            pieces = [
                fland[0, s, sc, :, t * deep : (t + 1) * deep]
                + fland[1, s, sc, :, t * deep : (t + 1) * deep]
                for t in range(j * per_share, (j + 1) * per_share)
                for sc in range(splits)
            ]
            value = jnp.concatenate(pieces, axis=1)
            choice = value if choice is None else jnp.where(here == j, value, choice)
        row = lax.broadcasted_iota(jnp.int32, (deep, width), 0) + (me * own + s * deep)
        col = lax.broadcasted_iota(jnp.int32, (deep, width), 1) + column * width
        out_ref[s * deep : (s + 1) * deep, :] = jnp.where(row == col, 0.0, choice) * scale


def body(coeffs):
    parts, tapers, own, bins = coeffs.shape
    n = lax.axis_size("chan")
    groups = lax.axis_size("band")
    full = own * n
    m = n // 4
    hubs = 2 * m
    lanes = bins // hubs
    bands = lanes // W
    depth = parts * tapers * W
    strip = LANE
    strips = full // strip
    splits = strips // 4
    windows = lanes // LANE
    subs = SUBS
    slab = strip // subs
    members = groups * m
    shares = groups // 4
    scale = W * tapers / (bins // W * groups)
    dma = pltpu.SemaphoreType.DMA

    def run(*refs):
        kernel(scale, *refs)

    return pl.pallas_call(
        run,
        out_shape=pltpu.VMEM((own, full // groups), jnp.float32),
        in_specs=[pl.BlockSpec(memory_space=pl.ANY)],
        out_specs=pl.BlockSpec(memory_space=pltpu.VMEM),
        scratch_shapes=[
            pltpu.VMEM((strips, windows, parts, tapers, strip, LANE), jnp.bfloat16),
            pltpu.VMEM((tapers * LANE, LANE // W * depth // 2), jnp.bfloat16),
            pltpu.VMEM((bands, full, depth), jnp.bfloat16),
            pltpu.VMEM((LANE // W, 2 * slab, depth), jnp.bfloat16),
            pltpu.VMEM((slab, LANE), jnp.float32),
            pltpu.VMEM((strip, LANE), jnp.float32),
            pltpu.VMEM((bands, full), jnp.float32),
            pltpu.VMEM((strips, strips, subs, slab, strip), jnp.float32),
            pltpu.VMEM((strips, members, subs, slab, strip), jnp.float32),
            pltpu.VMEM((strips, 2, strip, strip), jnp.float32),
            pltpu.VMEM((2, splits, splits, strip // m, strip), jnp.float32),
            dma((2, m)),
            dma((strips, windows, subs)),
            dma((strips,)),
            dma((strips,)),
            dma((strips, 2, shares)),
            dma,
            pltpu.SemaphoreType.REGULAR,
            pltpu.SemaphoreType.REGULAR,
            pltpu.SemaphoreType.REGULAR,
        ],
        compiler_params=pltpu.CompilerParams(
            collective_id=0, has_side_effects=True, vmem_limit_bytes=56 * 1024 * 1024
        ),
    )(coeffs)


def solution(mesh):
    return jax.shard_map(
        body,
        mesh=mesh,
        in_specs=(P(None, None, "chan", "band"),),
        out_specs=P("chan", "band"),
        check_vma=False,
    )
```

time: 112 us -> 109 us (0.973)
  Pallas kernels: 110 us -> 107 us
    pallas_call x1, Pallas kernels: 110 us -> 107 us  [body(): pl.pallas_call(run, out_shape=pltpu.VMEM((own, full // groups), jnp.float...]
where the time goes in v3:
time: 109 us; the launch traced here: 108 us
  Pallas kernels  107 us (98%)
    pallas_call x1, Pallas kernels, body(): pl.pallas_call(run, out_shape=pltpu.VMEM((own, full // groups), jnp.float...  107 us

profile of v3, /device:TPU:0, one launch (start us, length us, event | category | flops | bytes accessed | tf_op | source)
XLA Modules:
  0.0 107.6 jit_solution(12522610434711411817)
XLA Ops:
  0.0 106.9 %shard_map.17 = f32[128,256]{1,0:T(8,128)S(1)} custom-call(bf16[2,8,128,1024]{3,2,1,0:T(8,128)(2,1)} %refs_0_.1), custom_call_target="tpu_custom_call" | custom-call | tf_op jit(solution)/shard_map/pallas_call | solution.py:448
  106.9 0.7 copy.3

commit v4 on v3

--- a/solution.py
+++ b/solution.py
@@ -374,6 +374,8 @@
             hit = (row == band * W + within - k * W) & (within // W == k)
             sel[k * LANE : (k + 1) * LANE, :] = jnp.where(hit, 1.0, 0.0).astype(jnp.bfloat16)
 
+        steps = strips * windows * subs
+
         def step(h, carry):
             w = lax.div(h, windows * subs)
             v = lax.rem(lax.div(h, subs), windows)
@@ -381,13 +383,17 @@
             pl.when((w > 0) & (v == windows - 1) & (i == 0))(lambda: reduce(w - 1))
             dst = buf.at[w, v, :, :, pl.ds(pl.multiple_of(i * slab, slab), slab), :]
             pltpu.make_async_copy(dst, dst, coef_recv.at[w, v, i]).wait()
+
+            @pl.when(h == steps - 1)
+            def _():
+                lax.fori_loop(quad, last, send_held, 0)
+
             relayout(w, v, i)
             gram(w, v, i)
             return carry
 
         meet()
-        lax.fori_loop(0, strips * windows * subs, step, 0)
-        lax.fori_loop(quad, last, send_held, 0)
+        lax.fori_loop(0, steps, step, 0)
         reduce(last)
         drain_parts()
         lax.fori_loop(0, strips, drain_tiles, 0)

time: 109 us -> 108 us (level)
  no operation moved by 1% of the time
where the time goes in v4:
time: 108 us
  Pallas kernels  107 us (99%)
    pallas_call x1, Pallas kernels, body(): pl.pallas_call(run, out_shape=pltpu.VMEM((own, full // groups), jnp.float...  107 us

profile of v4, /device:TPU:0, one launch (start us, length us, event | category | flops | bytes accessed | tf_op | source)
XLA Modules:
  0.0 107.6 jit_solution(12086275987008465747)
XLA Ops:
  0.0 106.9 %shard_map.17 = f32[128,256]{1,0:T(8,128)S(1)} custom-call(bf16[2,8,128,1024]{3,2,1,0:T(8,128)(2,1)} %refs_0_.1), custom_call_target="tpu_custom_call" | custom-call | tf_op jit(solution)/shard_map/pallas_call | solution.py:454
  107.0 0.7 copy.3

commit v5 on v4

--- a/solution.py
+++ b/solution.py
@@ -260,8 +260,8 @@
         def pair(k, carry):
             seat = jnp.where(
                 k == 0,
-                3 - at,
-                jnp.where(k == 1, lax.rem(at + 2, 4), jnp.where(k == 2, at + 1 - 2 * lax.rem(at, 2), at)),
+                at + 1 - 2 * lax.rem(at, 2),
+                jnp.where(k == 1, 3 - at, jnp.where(k == 2, lax.rem(at + 2, 4), at)),
             )
             u = quarter(side, seat)
 

time: 108 us -> 108 us (level)
  no operation moved by 1% of the time
where the time goes in v5:
time: 108 us
  Pallas kernels  107 us (99%)
    pallas_call x1, Pallas kernels, body(): pl.pallas_call(run, out_shape=pltpu.VMEM((own, full // groups), jnp.float...  107 us

profile of v5, /device:TPU:0, one launch (start us, length us, event | category | flops | bytes accessed | tf_op | source)
XLA Modules:
  0.0 108.1 jit_solution(12454710946884960798)
XLA Ops:
  0.0 107.4 %shard_map.17 = f32[128,256]{1,0:T(8,128)S(1)} custom-call(bf16[2,8,128,1024]{3,2,1,0:T(8,128)(2,1)} %refs_0_.1), custom_call_target="tpu_custom_call" | custom-call | tf_op jit(solution)/shard_map/pallas_call | solution.py:454
  107.4 0.7 copy.3
